TPU v7x, 32 devices: a whole 2x2x4 slice. The times are simulated.
32 devices in a mesh: groups: 2 (over x), rows: 16 (over z, y, core).
Axes of the slice: x: 2, y: 2, z: 4, core: 2. Of those that a mesh axis runs over, the one named last changes fastest.
Arguments:
- queries: bfloat16 [2048, 8192], P(('groups', 'rows')), parts along dimension 0, may hold values from -6 to 6
- sketches: bfloat16 [16384, 8192], P(('groups', 'rows')), parts along dimension 0, may hold values from -16 to 16, as said below
- row_ids: int32 [16384], P(('groups', 'rows')), parts along dimension 0, may hold values from 0 to 8191, each once
Outputs:
- top_scores: float32 [2048, 128], P(('groups', 'rows')), parts along dimension 0
There are 2 independent parts, one for each index of `groups`. A program takes and returns all parts, laid end to end along the dimension named above; each array names one. Nothing has to cross between parts.
Inputs may be any that keep to these rules, and one draw needn't show every extreme that they name: `sketches`: sketch entries are real-valued.
All inputs are finite; a program needn't handle non-finite values.
Results may differ from a plain program's by a relative error of at most 0.0003.
Values may be sent and summed in bfloat16 or wider, within the bound.
A program may use at most 128 MiB of HBM per device.

v0:
```python
import jax
import jax.numpy as jnp
from jax import lax
from jax.sharding import PartitionSpec as P

TOPK = 128


def shards(queries, sketches, row_ids):
    devices = lax.axis_size("rows")
    total_rows = sketches.shape[0] * devices
    retired = total_rows // 4
    live_count = total_rows - retired
    keep = TOPK
    scores = lax.dot_general(
        lax.all_gather(queries, "rows", axis=0, tiled=True),
        sketches,
        (((1,), (1,)), ((), ())),
        preferred_element_type=jnp.float32,
    )
    live = row_ids >= retired
    square_sum = jnp.sum(jnp.where(live[None, :], scores * scores, jnp.float32(0.0)), axis=1)
    masked = jnp.where(live[None, :], scores, jnp.float32(-1e30))
    candidates = lax.top_k(masked, keep)[0]
    payload = (candidates, square_sum[:, None])
    received = (
        lax.all_to_all(payload[0], "rows", split_axis=0, concat_axis=1, tiled=True),
        lax.all_to_all(payload[1], "rows", split_axis=0, concat_axis=1, tiled=True),
    )
    best = lax.top_k(received[0], keep)[0]
    own_sum = jnp.sum(received[1], axis=1)
    inverse_scale = lax.rsqrt(own_sum / jnp.float32(live_count) + jnp.float32(1e-06))
    return best * inverse_scale[:, None]


def solution(mesh):
    return jax.shard_map(
        shards,
        mesh=mesh,
        in_specs=(P(("groups", "rows"), None), P(("groups", "rows"), None), P(("groups", "rows"))),
        out_specs=P(("groups", "rows"), None),
        check_vma=False,
    )
```

profile of v0, /device:TPU:0, one launch (start us, length us, event | category | flops | bytes accessed | tf_op | source)
XLA Modules:
  0.0 261.9 jit_solution(8203778866880331875)
XLA Ops:
  6.5 0.0 all-gather.2.cloned.1.call-start
  6.5 0.7 all-gather.2.cloned.1.call-update
  7.3 0.7 broadcast_compare_fusion
  7.9 130.7 %all-gather.2.cloned.1.call-done = bf16[1024,8192]{1,0:T(8,128)(2,1)} async-done(((bf16[64,8192]{1,0:T(8,128)(2,1)}), bf16[1024,8192]{1,0:T(8,128)(2,1)}) %all-gather.2.cloned.1.call-update) | async-done | bytes 16777232 | tf_op jit(solution)/shard_map/all_gather | solution.py:16
  138.7 15.9 %select_reduce_fusion = (f32[1024]{0:T(1024)S(1)}, f32[1024,512]{0,1:T(8,128)}) fusion(pred[512]{0:T(512)(128)(4,1)S(1)} %broadcast_compare_fusion, bf16[1024,8192]{1,0:T(8,128)(2,1)} %all-gather.2.cloned.1.call-done, bf16[512,8192]{1,0:T(8,128)(2,1)} %param.4), kind=kOutput, calls=%fused_computation | convolution fusion | flops 8592030720 | bytes 27267584 | tf_op jit(solution)/shard_map/dot_general | solution.py:15
  154.5 0.7 all_to_all.28
  155.2 3.5 %all-to-all-start.1 = ((f32[16,64,1]{1,2,0:T(1,128)}), f32[16,64,1]{1,2,0:T(1,128)S(1)}, u32[]{:S(2)}, u32[]{:S(2)}) async-start(f32[16,64,1]{1,2,0:T(1,128)} %bitcast.2), calls=%async_computation.1 | async-start | bytes 16384 | tf_op jit(solution)/shard_map/all_to_all | solution.py:28
  158.7 0.1 iota.6.clone
  158.8 58.5 %top_k.14 = (f32[1024,512]{0,1:T(8,128)}, s32[1024,512]{0,1:T(8,128)}) sort(f32[1024,512]{0,1:T(8,128)} %get-tuple-element.15, s32[1024,512]{0,1:T(8,128)S(1)} %iota.6.clone), dimensions={1}, to_apply=%region_0.1 | sort | flops 9961472 | bytes 8388608 | tf_op jit(solution)/shard_map/top_k | solution.py:24
  217.3 1.9 copy.11
  219.3 0.9 top_k.22
  220.1 0.0 all-to-all-done.1
  220.1 6.0 %all-to-all-start = ((f32[16,64,128]{2,1,0:T(8,128)}), f32[16,64,128]{2,1,0:T(8,128)S(1)}, u32[]{:S(2)}, u32[]{:S(2)}) async-start(f32[16,64,128]{2,1,0:T(8,128)} %bitcast), calls=%async_computation | async-start | bytes 1048576 | tf_op jit(solution)/shard_map/all_to_all | solution.py:27
  226.2 14.2 %all-to-all-done = f32[16,64,128]{2,1,0:T(8,128)S(1)} async-done(((f32[16,64,128]{2,1,0:T(8,128)}), f32[16,64,128]{2,1,0:T(8,128)S(1)}, u32[]{:S(2)}, u32[]{:S(2)}) %all-to-all-start) | async-done | bytes 524320 | tf_op jit(solution)/shard_map/all_to_all | solution.py:27
  240.4 14.0 %sort_prefixfusion = f32[64,128]{1,0:T(8,128)S(1)} fusion(f32[64,2048]{1,0:T(8,128)S(1)} %copy_bitcast_fusion), kind=kCustom, calls=%top_k.20.sort_prefix | custom fusion | flops 2228224 | bytes 557056 | tf_op jit(solution)/shard_map/top_k | solution.py:30
  254.4 0.7 broadcast_multiply_fusion
  (3 shorter events, 0.1 us)
Async XLA Ops:
  6.5 132.1 %all-gather.2.cloned.1.call-start = ((), (), s32[]{:S(2)}) async-start(), calls=%async_computation.2 | async-start | bytes 17825792 | tf_op jit(solution)/shard_map/all_gather | solution.py:16
  155.2 64.9 %all-to-all-start.1 = ((f32[16,64,1]{1,2,0:T(1,128)}), f32[16,64,1]{1,2,0:T(1,128)S(1)}, u32[]{:S(2)}, u32[]{:S(2)}) async-start(f32[16,64,1]{1,2,0:T(1,128)} %bitcast.2), calls=%async_computation.1 | async-start | bytes 16384 | tf_op jit(solution)/shard_map/all_to_all | solution.py:28
  220.1 20.2 %all-to-all-start = ((f32[16,64,128]{2,1,0:T(8,128)}), f32[16,64,128]{2,1,0:T(8,128)S(1)}, u32[]{:S(2)}, u32[]{:S(2)}) async-start(f32[16,64,128]{2,1,0:T(8,128)} %bitcast), calls=%async_computation | async-start | bytes 1048576 | tf_op jit(solution)/shard_map/all_to_all | solution.py:27
Sparse Core Ops, SparseCore 0:
  9.5 129.1 all-gather.1
where the time goes:
time: 262 us
  waiting for transfers between devices  146 us (56%)
  other arithmetic  73.9 us (28%)
  matrix products  15.9 us (6%)
  between operations  13.4 us (5%)
  starting transfers between devices  9.45 us (4%)
  local copies, waits for them, and re-layouts  3.62 us (1%)
    all_gather x1, waiting for transfers between devices, shards(): lax.all_gather(queries, 'rows', axis=0, tiled=True)  131 us
    top_k x1, other arithmetic, shards(): candidates = lax.top_k(masked, keep)[0]  58.5 us
    dot_general x1, matrix products, shards(): lax.dot_general(lax.all_gather(queries, 'rows', axis=0, tiled=True), sket...  15.9 us
    all_to_all x1, waiting for transfers between devices, shards(): lax.all_to_all(payload[0], 'rows', split_axis=0, concat_axis=1, tiled=True)  14.2 us
    top_k x1, other arithmetic, shards(): best = lax.top_k(received[0], keep)[0]  14 us
    all_to_all x1, starting transfers between devices, shards(): lax.all_to_all(payload[0], 'rows', split_axis=0, concat_axis=1, tiled=True)  5.98 us
  transfers between devices with their start and end apart: 3, of which 2 were waited for; matrix products, arithmetic and copies ran while one was open for 24% of the time, Pallas kernels for 0%

commit v1 on v0

--- a/solution.py
+++ b/solution.py
@@ -7,6 +7,14 @@
 
 
 def shards(queries, sketches, row_ids):
+
+    def shape_targets(point, bus_axis):
+        vec_out = lax.axis_size(bus_axis)
+        newest = jnp.split(point, vec_out, 0)
+        main = jnp.stack(newest, 0)
+        y_new = lax.all_to_all(main, bus_axis, 0, 0)
+        return jnp.concatenate(y_new, 1)
+
     devices = lax.axis_size("rows")
     total_rows = sketches.shape[0] * devices
     retired = total_rows // 4
@@ -24,7 +32,7 @@
     candidates = lax.top_k(masked, keep)[0]
     payload = (candidates, square_sum[:, None])
     received = (
-        lax.all_to_all(payload[0], "rows", split_axis=0, concat_axis=1, tiled=True),
+        shape_targets(payload[0], "rows"),
         lax.all_to_all(payload[1], "rows", split_axis=0, concat_axis=1, tiled=True),
     )
     best = lax.top_k(received[0], keep)[0]

time: 262 us -> 271 us (1.034)
  local copies, waits for them, and re-layouts: 3.62 us -> 12.5 us
    unnamed x0 -> x15, local copies, waits for them, and re-layouts: none -> 9.1 us
  transfers between devices with their start and end apart: 3 -> 3, of which waited for: 2 -> 2; matrix products, arithmetic and copies ran while one was open for 24% -> 26% of each run, Pallas kernels for 0% -> 0%
where the time goes in v1:
time: 271 us
  waiting for transfers between devices  146 us (54%)
  other arithmetic  73.9 us (27%)
  matrix products  15.9 us (6%)
  between operations  13.4 us (5%)
  local copies, waits for them, and re-layouts  12.5 us (5%)
  starting transfers between devices  9.45 us (3%)
    all_gather x1, waiting for transfers between devices, shards(): lax.all_gather(queries, 'rows', axis=0, tiled=True)  131 us
    top_k x1, other arithmetic, shards(): candidates = lax.top_k(masked, keep)[0]  58.5 us
    dot_general x1, matrix products, shards(): lax.dot_general(lax.all_gather(queries, 'rows', axis=0, tiled=True), sket...  15.9 us
    all_to_all x1, waiting for transfers between devices, shape_targets(): y_new = lax.all_to_all(main, bus_axis, 0, 0)  14.2 us
    top_k x1, other arithmetic, shards(): best = lax.top_k(received[0], keep)[0]  14 us
    unnamed x15, local copies, waits for them, and re-layouts  9.1 us
    all_to_all x1, starting transfers between devices, shape_targets(): y_new = lax.all_to_all(main, bus_axis, 0, 0)  5.98 us
  transfers between devices with their start and end apart: 3, of which 2 were waited for; matrix products, arithmetic and copies ran while one was open for 26% of the time, Pallas kernels for 0%

profile of v1, /device:TPU:0, one launch (start us, length us, event | category | flops | bytes accessed | tf_op | source)
XLA Modules:
  0.0 270.8 jit_solution(6565948817199451901)
XLA Ops:
  6.5 0.7 all-gather.2.cloned.1.call-update
  7.3 0.7 broadcast_compare_fusion
  7.9 130.7 %all-gather.2.cloned.1.call-done = bf16[1024,8192]{1,0:T(8,128)(2,1)} async-done(((bf16[64,8192]{1,0:T(8,128)(2,1)}), bf16[1024,8192]{1,0:T(8,128)(2,1)}) %all-gather.2.cloned.1.call-update) | async-done | bytes 16777232 | tf_op jit(solution)/shard_map/all_gather | solution.py:24
  138.7 15.9 %select_reduce_fusion = (f32[1024]{0:T(1024)S(1)}, f32[1024,512]{0,1:T(8,128)}) fusion(pred[512]{0:T(512)(128)(4,1)S(1)} %broadcast_compare_fusion, bf16[1024,8192]{1,0:T(8,128)(2,1)} %all-gather.2.cloned.1.call-done, bf16[512,8192]{1,0:T(8,128)(2,1)} %param.4), kind=kOutput, calls=%fused_computation | convolution fusion | flops 8592030720 | bytes 27267584 | tf_op jit(solution)/shard_map/dot_general | solution.py:23
  154.5 0.7 all_to_all.14
  155.2 3.5 %all-to-all-start.1 = ((f32[16,64,1]{1,2,0:T(1,128)}), f32[16,64,1]{1,2,0:T(1,128)S(1)}, u32[]{:S(2)}, u32[]{:S(2)}) async-start(f32[16,64,1]{1,2,0:T(1,128)} %bitcast.17), calls=%async_computation.1 | async-start | bytes 16384 | tf_op jit(solution)/shard_map/all_to_all | solution.py:36
  158.8 58.5 %top_k.13 = (f32[1024,512]{0,1:T(8,128)}, s32[1024,512]{0,1:T(8,128)}) sort(f32[1024,512]{0,1:T(8,128)} %get-tuple-element.15, s32[1024,512]{0,1:T(8,128)S(1)} %iota.6.clone), dimensions={1}, to_apply=%region_0.1 | sort | flops 9961472 | bytes 8388608 | tf_op jit(solution)/shard_map/top_k | solution.py:32
  217.3 1.9 copy.11
  219.3 0.6 constant_dynamic-update-slice_fusion.15
  219.9 0.6 constant_dynamic-update-slice_fusion.14
  221.1 0.6 constant_dynamic-update-slice_fusion.12
  222.3 0.6 constant_dynamic-update-slice_fusion.10
  222.9 0.6 constant_dynamic-update-slice_fusion.9
  223.5 0.6 constant_dynamic-update-slice_fusion.8
  224.7 0.6 constant_dynamic-update-slice_fusion.6
  225.3 0.6 constant_dynamic-update-slice_fusion.5
  226.0 0.6 constant_dynamic-update-slice_fusion.4
  226.6 0.6 constant_dynamic-update-slice_fusion.3
  227.2 0.6 constant_dynamic-update-slice_fusion.2
  227.8 0.6 constant_dynamic-update-slice_fusion.1
  229.0 6.0 %all-to-all-start = ((f32[16,64,128]{2,1,0:T(8,128)}), f32[16,64,128]{2,1,0:T(8,128)S(1)}, u32[]{:S(2)}, u32[]{:S(2)}) async-start(f32[16,64,128]{2,1,0:T(8,128)} %constant_dynamic-update-slice_fusion), calls=%async_computation | async-start | bytes 1048576 | tf_op jit(solution)/shard_map/all_to_all | solution.py:15
  235.0 14.2 %all-to-all-done = f32[16,64,128]{2,1,0:T(8,128)S(1)} async-done(((f32[16,64,128]{2,1,0:T(8,128)}), f32[16,64,128]{2,1,0:T(8,128)S(1)}, u32[]{:S(2)}, u32[]{:S(2)}) %all-to-all-start) | async-done | bytes 524320 | tf_op jit(solution)/shard_map/all_to_all | solution.py:15
  249.3 14.0 %sort_prefixfusion = f32[64,128]{1,0:T(8,128)S(1)} fusion(f32[64,2048]{1,0:T(8,128)S(1)} %copy_bitcast_fusion), kind=kCustom, calls=%top_k.14.sort_prefix | custom fusion | flops 2228224 | bytes 557056 | tf_op jit(solution)/shard_map/top_k | solution.py:38
  263.3 0.7 broadcast_multiply_fusion
  (10 shorter events, 2.6 us)
Async XLA Ops:
  6.5 132.1 %all-gather.2.cloned.1.call-start = ((), (), s32[]{:S(2)}) async-start(), calls=%async_computation.2 | async-start | bytes 17825792 | tf_op jit(solution)/shard_map/all_gather | solution.py:24
  155.2 73.8 %all-to-all-start.1 = ((f32[16,64,1]{1,2,0:T(1,128)}), f32[16,64,1]{1,2,0:T(1,128)S(1)}, u32[]{:S(2)}, u32[]{:S(2)}) async-start(f32[16,64,1]{1,2,0:T(1,128)} %bitcast.17), calls=%async_computation.1 | async-start | bytes 16384 | tf_op jit(solution)/shard_map/all_to_all | solution.py:36
  229.0 20.2 %all-to-all-start = ((f32[16,64,128]{2,1,0:T(8,128)}), f32[16,64,128]{2,1,0:T(8,128)S(1)}, u32[]{:S(2)}, u32[]{:S(2)}) async-start(f32[16,64,128]{2,1,0:T(8,128)} %constant_dynamic-update-slice_fusion), calls=%async_computation | async-start | bytes 1048576 | tf_op jit(solution)/shard_map/all_to_all | solution.py:15
Sparse Core Ops, SparseCore 0:
  9.5 129.1 all-gather.1
